TPU v7x, 32 devices: a whole 2x2x4 slice. The times are simulated.
32 devices in a mesh: dp: 8 (over z, y), tensor: 4 (over x, core).
Axes of the slice: x: 2, y: 2, z: 4, core: 2. Of those that a mesh axis runs over, the one named last changes fastest.
Arguments:
- tokens: bfloat16 [8704, 1024], P(('dp', 'tensor')), may hold values from -6 to 6
- text_lengths: int32 [8], P('dp'), may hold values from 1 to 64, as said below
- norm1_gain: float32 [1024], replicated, may hold values from 0.25 to 1.75
- norm1_shift: float32 [1024], replicated, may hold values from -1.75 to 1.75
- w_qkv: bfloat16 [1024, 3072], P(None, 'tensor'), may hold values from -0.25 to 0.25
- q_bias: float32 [1024], P('tensor'), may hold values from -1.75 to 1.75
- v_bias: float32 [1024], P('tensor'), may hold values from -1.75 to 1.75
- w_out: bfloat16 [1024, 1024], P('tensor'), may hold values from -1 to 1
- out_bias: float32 [1024], replicated, may hold values from -1.75 to 1.75
- norm2_gain: float32 [1024], replicated, may hold values from 0.25 to 1.75
- norm2_shift: float32 [1024], replicated, may hold values from -1.75 to 1.75
- norm3_gain: float32 [1024], replicated, may hold values from 0.25 to 1.75
- norm3_shift: float32 [1024], replicated, may hold values from -1.75 to 1.75
- w_fc1: bfloat16 [1024, 4096], P(None, 'tensor'), may hold values from -0.1875 to 0.1875
- fc1_bias: bfloat16 [4096], P('tensor'), may hold values from -3 to 3
- w_fc2: bfloat16 [4096, 1024], P('tensor'), may hold values from -0.09375 to 0.09375
- fc2_bias: float32 [1024], replicated, may hold values from -1.75 to 1.75
- norm4_gain: float32 [1024], replicated, may hold values from 0.25 to 1.75
- norm4_shift: float32 [1024], replicated, may hold values from -1.75 to 1.75
- cotangent: bfloat16 [8704, 1024], P(('dp', 'tensor')), may hold values from -16 to 16
Outputs:
- layer_out: bfloat16 [8704, 1024], P(('dp', 'tensor'))
- input_grad: float32 [8704, 1024], P(('dp', 'tensor'))
- grad_norm1_gain: float32 [1024], replicated
- grad_norm1_shift: float32 [1024], replicated
- grad_qkv: float32 [1024, 3072], P(None, 'tensor')
- grad_q_bias: float32 [1024], P('tensor')
- grad_v_bias: float32 [1024], P('tensor')
- grad_out: float32 [1024, 1024], P('tensor')
- grad_out_bias: float32 [1024], replicated
- grad_norm2_gain: float32 [1024], replicated
- grad_norm2_shift: float32 [1024], replicated
- grad_norm3_gain: float32 [1024], replicated
- grad_norm3_shift: float32 [1024], replicated
- grad_fc1: float32 [1024, 4096], P(None, 'tensor')
- grad_fc1_bias: float32 [4096], P('tensor')
- grad_fc2: float32 [4096, 1024], P('tensor')
- grad_fc2_bias: float32 [1024], replicated
- grad_norm4_gain: float32 [1024], replicated
- grad_norm4_shift: float32 [1024], replicated
Inputs may be any that keep to these rules, and one draw needn't show every extreme that they name: `text_lengths`: some sequence has all 64 text positions real and some has only one.
All inputs are finite; a program needn't handle non-finite values.
Results may differ from a plain program's by a relative error of at most 0.014.
The roundings to bfloat16 on the way count: a program that leaves them out, or rounds other values in their place, can miss the bound.
Values may be sent and summed in bfloat16 or wider, within the bound.
A program may use at most 192 MiB of HBM per device.

v0:
```python
from functools import partial
import math

import jax
import jax.numpy as jnp
from jax import lax
from jax.sharding import PartitionSpec as P

HD = 64
TEXT = 64
ALPHA = 32
LEN = 1088


epsilon = 1e-05


def times_transposed(left, right):
    return lax.dot_general(
        left, right, (((1,), (1,)), ((), ())), preferred_element_type=jnp.float32
    )


def transposed_times(left, right):
    return lax.dot_general(
        left, right, (((0,), (0,)), ((), ())), preferred_element_type=jnp.float32
    )


def norm_forward(values, norm_gain, norm_shift):
    centre = jnp.mean(values, axis=-1, keepdims=True)
    centered = values - centre
    inverse = lax.rsqrt(jnp.mean(centered * centered, axis=-1, keepdims=True) + epsilon)
    normed = centered * inverse
    return (normed * norm_gain + norm_shift, normed, inverse)


def norm_backward(grad_out, normed, inverse, norm_gain):
    scaled = grad_out * norm_gain
    inner_term = (
        scaled
        - jnp.mean(scaled, axis=-1, keepdims=True)
        - normed * jnp.mean(scaled * normed, axis=-1, keepdims=True)
    )
    return (inner_term * inverse, jnp.sum(grad_out * normed, axis=0), jnp.sum(grad_out, axis=0))


def gelu_back(inner_act, grad_act):
    _, pullback = jax.vjp(partial(jax.nn.gelu, approximate=True), inner_act)
    return pullback(grad_act)[0]


def masked_scores(query_rows, key_rows, length):
    seq_len = query_rows.shape[0]
    scores_raw = jnp.einsum(
        "qhd,khd->hqk", query_rows, key_rows, preferred_element_type=jnp.float32
    )
    scaled = scores_raw / (ALPHA * math.sqrt(HD))
    query_pos = lax.broadcasted_iota(jnp.int32, (seq_len, seq_len), 0)
    key_pos = lax.broadcasted_iota(jnp.int32, (seq_len, seq_len), 1)
    is_valid = ((key_pos <= query_pos) & ((key_pos >= TEXT) | (key_pos < length)))[None]
    return (jnp.where(is_valid, scaled, -1e30), is_valid)


def attend_forward(inputs):
    query_rows, key_rows, value_rows, length = inputs
    masked, is_valid = masked_scores(query_rows, key_rows, length)
    row_top = jnp.max(masked, axis=-1, keepdims=True)
    exponent = jnp.where(is_valid, jnp.exp(ALPHA * (masked - row_top)), 0.0)
    row_total = jnp.sum(exponent, axis=-1, keepdims=True)
    weights_low = (exponent / row_total).astype(jnp.bfloat16)
    context = jnp.einsum(
        "hqk,khd->qhd", weights_low, value_rows, preferred_element_type=jnp.float32
    )
    return (context, row_top, row_total)


def attend_backward(inputs):
    query_rows, key_rows, value_rows, length, grad_context, row_top, row_total = inputs
    masked, is_valid = masked_scores(query_rows, key_rows, length)
    weights_soft = jnp.where(is_valid, jnp.exp(ALPHA * (masked - row_top)), 0.0) / row_total
    grad_values = jnp.einsum(
        "hqk,qhd->khd",
        weights_soft.astype(jnp.bfloat16),
        grad_context,
        preferred_element_type=jnp.float32,
    )
    grad_soft = jnp.einsum(
        "qhd,khd->hqk", grad_context, value_rows, preferred_element_type=jnp.float32
    )
    grad_expon = weights_soft * (
        grad_soft - jnp.sum(weights_soft * grad_soft, axis=-1, keepdims=True)
    )
    grad_scores = (grad_expon * ALPHA / (ALPHA * math.sqrt(HD))).astype(jnp.bfloat16)
    grad_queries = jnp.einsum(
        "hqk,khd->qhd", grad_scores, key_rows, preferred_element_type=jnp.float32
    )
    grad_keys = jnp.einsum(
        "hqk,qhd->khd", grad_scores, query_rows, preferred_element_type=jnp.float32
    )
    return (
        grad_queries.astype(jnp.bfloat16),
        grad_keys.astype(jnp.bfloat16),
        grad_values.astype(jnp.bfloat16),
    )


def local(
    tokens,
    text_lengths,
    norm1_gain,
    norm1_shift,
    w_qkv,
    q_bias,
    v_bias,
    w_out,
    out_bias,
    norm2_gain,
    norm2_shift,
    norm3_gain,
    norm3_shift,
    w_fc1,
    fc1_bias,
    w_fc2,
    fc2_bias,
    norm4_gain,
    norm4_shift,
    cotangent,
):
    seq_dev = text_lengths.shape[0]
    local_heads = q_bias.shape[0] // HD
    rows_all = seq_dev * LEN
    input_rows = tokens.astype(jnp.float32)
    first_out, first_hat, first_inv = norm_forward(input_rows, norm1_gain, norm1_shift)
    gathered_first = lax.all_gather(first_out.astype(jnp.bfloat16), "tensor", axis=0, tiled=True)
    projected = jnp.dot(gathered_first, w_qkv, preferred_element_type=jnp.float32).reshape(
        rows_all, local_heads, 3, HD
    )
    seq_shape = (seq_dev, LEN, local_heads, HD)
    query_rows = (
        (projected[:, :, 0] + q_bias.reshape(local_heads, HD))
        .astype(jnp.bfloat16)
        .reshape(seq_shape)
    )
    key_rows = projected[:, :, 1].astype(jnp.bfloat16).reshape(seq_shape)
    value_rows = (
        (projected[:, :, 2] + v_bias.reshape(local_heads, HD))
        .astype(jnp.bfloat16)
        .reshape(seq_shape)
    )
    context, row_tops, row_totals = lax.map(
        attend_forward, (query_rows, key_rows, value_rows, text_lengths)
    )
    context_low = context.reshape(rows_all, local_heads * HD).astype(jnp.bfloat16)
    branch = (
        lax.psum_scatter(
            jnp.dot(context_low, w_out, preferred_element_type=jnp.float32),
            "tensor",
            scatter_dimension=0,
            tiled=True,
        )
        + out_bias
    )
    second_out, second_hat, second_inv = norm_forward(branch, norm2_gain, norm2_shift)
    hidden = input_rows + second_out
    third_out, third_hat, third_inv = norm_forward(hidden, norm3_gain, norm3_shift)
    third_low = third_out.astype(jnp.bfloat16)
    gathered_third = lax.all_gather(third_low, "tensor", axis=0, tiled=True)
    inner_act = jnp.dot(gathered_third, w_fc1, preferred_element_type=jnp.float32) + fc1_bias
    activated = jax.nn.gelu(inner_act, approximate=True).astype(jnp.bfloat16)
    mixed_out = (
        lax.psum_scatter(
            jnp.dot(activated, w_fc2, preferred_element_type=jnp.float32),
            "tensor",
            scatter_dimension=0,
            tiled=True,
        )
        + fc2_bias
    )
    fourth_out, fourth_hat, fourth_inv = norm_forward(mixed_out, norm4_gain, norm4_shift)
    layer_out = (hidden + fourth_out).astype(jnp.bfloat16)
    grad_rows = cotangent.astype(jnp.float32)
    grad_mixed, grad_gain4, grad_shift4 = norm_backward(
        grad_rows, fourth_hat, fourth_inv, norm4_gain
    )
    mixed_low = grad_mixed.astype(jnp.bfloat16)
    grad_fc2_bias = jnp.sum(mixed_low, axis=0, dtype=jnp.float32)
    gathered_grad = lax.all_gather(mixed_low, "tensor", axis=0, tiled=True)
    grad_activated = times_transposed(gathered_grad, w_fc2)
    ffn_fc2 = transposed_times(activated, gathered_grad)
    grad_inner = gelu_back(inner_act, grad_activated).astype(jnp.bfloat16)
    ffn_fc1_bias = jnp.sum(grad_inner, axis=0, dtype=jnp.float32)
    ffn_fc1 = transposed_times(gathered_third, grad_inner)
    grad_third = lax.psum_scatter(
        times_transposed(grad_inner, w_fc1), "tensor", scatter_dimension=0, tiled=True
    )
    grad_mid_norm, grad_gain3, grad_shift3 = norm_backward(
        grad_third, third_hat, third_inv, norm3_gain
    )
    grad_hidden = grad_rows + grad_mid_norm
    grad_branch, grad_gain2, grad_shift2 = norm_backward(
        grad_hidden, second_hat, second_inv, norm2_gain
    )
    branch_low = grad_branch.astype(jnp.bfloat16)
    grad_out_bias = jnp.sum(branch_low, axis=0, dtype=jnp.float32)
    gathered_branch = lax.all_gather(branch_low, "tensor", axis=0, tiled=True)
    grad_context = times_transposed(gathered_branch, w_out).astype(jnp.bfloat16).reshape(seq_shape)
    part_out = transposed_times(context_low, gathered_branch)
    grad_queries, grad_keys, grad_values = lax.map(
        attend_backward,
        (query_rows, key_rows, value_rows, text_lengths, grad_context, row_tops, row_totals),
    )
    part_q_bias = jnp.sum(grad_queries, axis=(0, 1), dtype=jnp.float32).reshape(local_heads * HD)
    part_v_bias = jnp.sum(grad_values, axis=(0, 1), dtype=jnp.float32).reshape(local_heads * HD)
    grad_projected = jnp.stack([grad_queries, grad_keys, grad_values], axis=3).reshape(
        rows_all, 3 * local_heads * HD
    )
    part_qkv = transposed_times(gathered_first, grad_projected)
    grad_first = lax.psum_scatter(
        times_transposed(grad_projected, w_qkv), "tensor", scatter_dimension=0, tiled=True
    )
    grad_input_norm, grad_gain1, grad_shift1 = norm_backward(
        grad_first, first_hat, first_inv, norm1_gain
    )
    input_grad = grad_hidden + grad_input_norm
    (
        grad_gain1,
        grad_shift1,
        grad_gain2,
        grad_shift2,
        grad_gain3,
        grad_shift3,
        grad_gain4,
        grad_shift4,
        grad_out_bias,
        grad_fc2_bias,
    ) = lax.psum(
        (
            grad_gain1,
            grad_shift1,
            grad_gain2,
            grad_shift2,
            grad_gain3,
            grad_shift3,
            grad_gain4,
            grad_shift4,
            grad_out_bias,
            grad_fc2_bias,
        ),
        ("dp", "tensor"),
    )
    part_qkv, part_q_bias, part_v_bias, part_out, ffn_fc1, ffn_fc1_bias, ffn_fc2 = lax.psum(
        (part_qkv, part_q_bias, part_v_bias, part_out, ffn_fc1, ffn_fc1_bias, ffn_fc2), "dp"
    )
    return (
        layer_out,
        input_grad,
        grad_gain1,
        grad_shift1,
        part_qkv,
        part_q_bias,
        part_v_bias,
        part_out,
        grad_out_bias,
        grad_gain2,
        grad_shift2,
        grad_gain3,
        grad_shift3,
        ffn_fc1,
        ffn_fc1_bias,
        ffn_fc2,
        grad_fc2_bias,
        grad_gain4,
        grad_shift4,
    )


def solution(mesh):
    in_specs = (
        P(("dp", "tensor"), None),
        P("dp"),
        P(),
        P(),
        P(None, "tensor"),
        P("tensor"),
        P("tensor"),
        P("tensor", None),
        P(),
        P(),
        P(),
        P(),
        P(),
        P(None, "tensor"),
        P("tensor"),
        P("tensor", None),
        P(),
        P(),
        P(),
        P(("dp", "tensor"), None),
    )
    out_specs = (
        P(("dp", "tensor"), None),
        P(("dp", "tensor"), None),
        P(),
        P(),
        P(None, "tensor"),
        P("tensor"),
        P("tensor"),
        P("tensor", None),
        P(),
        P(),
        P(),
        P(),
        P(),
        P(None, "tensor"),
        P("tensor"),
        P("tensor", None),
        P(),
        P(),
        P(),
    )
    return jax.shard_map(local, mesh=mesh, in_specs=in_specs, out_specs=out_specs, check_vma=False)
```

profile of v0, /device:TPU:0, one launch (start us, length us, event | category | flops | bytes accessed | tf_op | source)
XLA Modules:
  0.0 873.2 jit_solution(11347173532757711064)
XLA Ops:
  10.6 2.1 fusion.59
  14.1 24.9 %all-gather.5.cloned.1.call-done = bf16[1088,1024]{1,0:T(8,128)(2,1)} async-done(((bf16[272,1024]{1,0:T(8,128)(2,1)}), bf16[1088,1024]{1,0:T(8,128)(2,1)}) %all-gather.5.cloned.1.call-update) | async-done | bytes 2228240 | tf_op jit(solution)/shard_map/all_gather | solution.py:135
  39.0 6.1 fusion.96
  45.1 15.5 %fusion.89 = (f32[4,1088]{1,0:T(4,128)S(1)}, f32[4,1088,1088]{1,2,0:T(8,128)}) fusion(pred[1088,1088]{0,1:T(8,128)(4,1)S(1)} %fusion.22, f32[1088,4,3,64]{0,3,2,1:T(8,128)} %bitcast.78, f32[4,64]{1,0:T(4,128)S(1)} %add.181), kind=kOutput, calls=%fused_computation.128 | convolution fusion | flops 635044928 | bytes 23235584 | tf_op jit(solution)/shard_map/while/body/eval_jaxpr/sub | solution.py:69
  60.6 9.0 %fusion.30 = bf16[4,64,1088]{2,1,0:T(8,128)(2,1)S(1)} fusion(f32[1088,4,3,64]{0,3,2,1:T(8,128)} %bitcast.79, f32[4,64]{1,0:T(4,128)S(1)} %add.178, f32[4,1088,1088]{1,2,0:T(8,128)} %get-tuple-element.120, f32[4,1088]{1,0:T(4,128)S(1)} %get-tuple-element.119), kind=kOutput, calls=%fused_computation.35 | convolution fusion | flops 616382464 | bytes 21809152 | tf_op jit(solution)/shard_map/while/body/eval_jaxpr/hqk,khd->qhd/dot_general | solution.py:72
  70.4 2.8 fusion.97
  73.3 10.2 %all-gather.7.cloned.1.call-start = ((), (), s32[]{:S(2)}) async-start(), calls=%async_computation.6 | async-start | bytes 2785280 | tf_op jit(solution)/shard_map/all_gather | solution.py:168
  83.5 36.2 %reduce-scatter.5.cloned.1.call-done = f32[272,1024]{1,0:T(8,128)} async-done(((f32[1088,1024]{1,0:T(8,128)}), f32[272,1024]{1,0:T(8,128)}) %reduce-scatter.5.cloned.1.call-update) | async-done | bytes 1114128 | tf_op jit(solution)/shard_map/reduce_scatter | solution.py:156
  123.6 23.4 %all-gather.7.cloned.1.call-done = bf16[1088,1024]{1,0:T(8,128)(2,1)} async-done(((bf16[272,1024]{1,0:T(8,128)(2,1)}), bf16[1088,1024]{1,0:T(8,128)(2,1)}) %all-gather.7.cloned.1.call-update) | async-done | bytes 2228240 | tf_op jit(solution)/shard_map/all_gather | solution.py:168
  147.0 4.7 convolution_add_fusion
  153.8 4.9 fusion.85
  158.8 46.3 %reduce-scatter.7.cloned.1.call-done = f32[272,1024]{1,0:T(8,128)} async-done(((f32[1088,1024]{1,0:T(8,128)}), f32[272,1024]{1,0:T(8,128)}) %reduce-scatter.7.cloned.1.call-update) | async-done | bytes 1114128 | tf_op jit(solution)/shard_map/reduce_scatter | solution.py:172
  209.5 23.4 %all-gather.9.cloned.1.call-done = bf16[1088,1024]{1,0:T(8,128)(2,1)} async-done(((bf16[272,1024]{1,0:T(8,128)(2,1)}), bf16[1088,1024]{1,0:T(8,128)(2,1)}) %all-gather.9.cloned.1.call-update) | async-done | bytes 2228240 | tf_op jit(solution)/shard_map/all_gather | solution.py:188
  232.9 7.8 convert_reduce_fusion
  242.0 4.6 fusion.98
  246.7 46.4 %reduce-scatter.9.cloned.1.call-done = f32[272,1024]{1,0:T(8,128)} async-done(((f32[1088,1024]{1,0:T(8,128)}), f32[272,1024]{1,0:T(8,128)}) %reduce-scatter.9.cloned.1.call-update) | async-done | bytes 1114128 | tf_op jit(solution)/shard_map/reduce_scatter | solution.py:194
  294.9 2.3 multiply_reduce_fusion.2
  299.0 23.0 %all-gather.11.cloned.1.call-done = bf16[1088,1024]{1,0:T(8,128)(2,1)} async-done(((bf16[272,1024]{1,0:T(8,128)(2,1)}), bf16[1088,1024]{1,0:T(8,128)(2,1)}) %all-gather.11.cloned.1.call-update) | async-done | bytes 2228240 | tf_op jit(solution)/shard_map/all_gather | solution.py:206
  322.0 2.4 convolution_convert_fusion
  324.7 9.8 %convert_reduce_fusion.3 = (f32[4,64]{1,0:T(4,128)S(1)}, bf16[4,64,1088]{2,1,0:T(8,128)(2,1)S(1)}) fusion(bf16[1088,4,64]{0,2,1:T(8,128)(2,1)S(1)} %bitcast.70, f32[4,1088,1088]{1,2,0:T(8,128)} %get-tuple-element.120, f32[4,1088]{1,0:T(4,128)S(1)} %get-tuple-element.119), kind=kOutput, calls=%fused_computation.65 | convolution fusion | flops 616382208 | bytes 20072448 | tf_op jit(solution)/shard_map/while/body/eval_jaxpr/hqk,qhd->khd/dot_general | solution.py:82
  334.5 10.9 %fusion.74 = f32[4,1088,1088]{1,2,0:T(8,128)} fusion(bf16[1088,4,64]{0,2,1:T(8,128)(2,1)S(1)} %bitcast.71, f32[1088,4,3,64]{0,3,2,1:T(8,128)} %bitcast.80, f32[4,64]{1,0:T(4,128)S(1)} %add.178), kind=kOutput, calls=%fused_computation.101 | convolution fusion | flops 606633984 | bytes 20677632 | tf_op jit(solution)/shard_map/while/body/eval_jaxpr/qhd,khd->hqk/dot_general | solution.py:88
  345.4 26.3 %fusion.42 = bf16[1,1088,4,1,64]{1,4,2,3,0:T(8,128)(2,1)S(1)} fusion(f32[4,1088,1088]{1,2,0:T(8,128)} %fusion.74, f32[1088,4,3,64]{0,3,2,1:T(8,128)} %bitcast.81, f32[4,64]{1,0:T(4,128)S(1)} %add.181, f32[4,1088,1088]{1,2,0:T(8,128)} %get-tuple-element.120, f32[4,1088]{1,0:T(4,128)S(1)} %get-tuple-element.119), kind=kOutput, calls=%fused_computation.40 | convolution fusion | flops 640062784 | bytes 81991680 | tf_op jit(solution)/shard_map/while/body/eval_jaxpr/hqk,qhd->khd/dot_general | solution.py:98
  371.7 27.5 %convert_reduce_fusion.4 = (f32[4,64]{1,0:T(4,128)S(1)}, bf16[4,64,1088]{2,1,0:T(8,128)(2,1)}) fusion(f32[4,1088,1088]{1,2,0:T(8,128)} %fusion.74, f32[4,1088,1088]{1,2,0:T(8,128)} %get-tuple-element.120, f32[4,1088]{1,0:T(4,128)S(1)} %get-tuple-element.119, f32[1088,4,3,64]{0,3,2,1:T(8,128)} %bitcast.82), kind=kOutput, calls=%fused_computation.66 | convolution fusion | flops 640062528 | bytes 81400832 | tf_op jit(solution)/shard_map/while/body/eval_jaxpr/hqk,khd->qhd/dot_general | solution.py:95
  402.5 4.2 fusion.99
  406.9 7.4 fusion.102
  414.4 8.7 fusion.84
  424.9 4.0 fusion.100
  429.0 22.4 %all-reduce.1 = (f32[256]{0:T(256)}, f32[256]{0:T(256)}, f32[1024]{0:T(1024)}) all-reduce(f32[256]{0:T(256)S(1)} %reshape.200, f32[256]{0:T(256)S(1)} %reshape.201, f32[1024]{0:T(1024)S(1)} %get-tuple-element.109), channel_id=1, replica_groups=mesh['dp'=8,'tensor'=4] {'dp'}, use_global_device_ids=true, to_apply=%region_29.30 | all-reduce | flops 1536 | bytes 12288 | tf_op jit(solution)/shard_map/psum | solution.py:252
  455.0 44.4 %all-reduce = (f32[1024]{0:T(1024)}, f32[1024]{0:T(1024)}, f32[1024]{0:T(1024)}, f32[1024]{0:T(1024)}, f32[1024]{0:T(1024)}, /*index=5*/f32[1024]{0:T(1024)}, f3...) all-reduce(f32[1024]{0:T(1024)S(1)} %get-tuple-element.82, ...), channel_id=1, replica_groups=mesh['dp'=8,'tensor'=4] {'dp','tensor'}, use_global_device_ids=true, to_apply=%region_24.25 | all-reduce | flops 10240 | bytes 81920 | tf_op jit(solution)/shard_map/psum | solution.py:237
  499.4 2.7 fusion.63
  502.1 352.7 %all-reduce.5.cloned.1.call-done = (f32[1024,768]{1,0:T(8,128)}, f32[256,1024]{1,0:T(8,128)}, f32[1024,1024]{1,0:T(8,128)}, f32[1024,1024]{1,0:T(8,128)}) async-done(((f32[1024,768]{1,0:T(8,128)}, f32[256,1024]{1,0:T(8,128)}, f32[1024,1024]{1,0:T(8,128)}, f32[1024,1024]{1,0:T(8,128)}), (f32[1024,768]{1,0:T(8,128)}, f32[256,1024]{1,0:T(8,128)}, f32[1024,1024]{1,0:T(8,128)}, ...) | async-done | bytes 12582928 | tf_op jit(solution)/shard_map/psum | solution.py:252
  854.7 3.9 copy.76
  (147 shorter events, 37.2 us)
Async XLA Ops:
  7.2 146.6 %copy-start = (bf16[1024,1024]{1,0:T(8,128)(2,1)S(1)}, bf16[1024,1024]{1,0:T(8,128)(2,1)}, u32[]{:S(2)}) copy-start(bf16[1024,1024]{1,0:T(8,128)(2,1)} %param.35) | copy-start | bytes 6291460
  7.2 6.3 copy-start.34
  7.2 6.4 copy-start.35
  7.2 31.8 %all-gather.5.cloned.1.call-start = ((), (), s32[]{:S(2)}) async-start(), calls=%async_computation.4 | async-start | bytes 2785280 | tf_op jit(solution)/shard_map/all_gather | solution.py:135
  12.8 106.9 %reduce-scatter.5.cloned.1.call-start = ((), (), s32[]{:S(2)}) async-start(), calls=%async_computation.5 | async-start | bytes 5570560 | tf_op jit(solution)/shard_map/reduce_scatter | solution.py:156
  60.6 9.8 %copy-start.18 = (bf16[256,1024]{1,0:T(8,128)(2,1)S(1)}, bf16[256,1024]{1,0:T(8,128)(2,1)}, u32[]{:S(2)}) copy-start(bf16[256,1024]{1,0:T(8,128)(2,1)} %param.27) | copy-start | bytes 1572868
  73.2 46.4 %copy-start.20 = (f32[1024]{0:T(1024)S(1)}, f32[1024]{0:T(1024)}, u32[]{:S(2)}) copy-start(f32[1024]{0:T(1024)} %param.28) | copy-start | bytes 12292
  73.3 48.3 %copy-start.26 = (f32[1024]{0:T(1024)S(1)}, f32[1024]{0:T(1024)}, u32[]{:S(2)}) copy-start(f32[1024]{0:T(1024)} %param.29) | copy-start | bytes 12292
  73.3 48.3 %copy-start.30 = (f32[1024]{0:T(1024)S(1)}, f32[1024]{0:T(1024)}, u32[]{:S(2)}) copy-start(f32[1024]{0:T(1024)} %param.30) | copy-start | bytes 12292
  73.3 73.7 %all-gather.7.cloned.1.call-start = ((), (), s32[]{:S(2)}) async-start(), calls=%async_computation.6 | async-start | bytes 2785280 | tf_op jit(solution)/shard_map/all_gather | solution.py:168
  123.5 81.6 %reduce-scatter.7.cloned.1.call-start = ((), (), s32[]{:S(2)}) async-start(), calls=%async_computation.7 | async-start | bytes 5570560 | tf_op jit(solution)/shard_map/reduce_scatter | solution.py:172
  158.7 46.4 %copy-start.21 = (f32[1024]{0:T(1024)S(1)}, f32[1024]{0:T(1024)}, u32[]{:S(2)}) copy-start(f32[1024]{0:T(1024)} %param.36) | copy-start | bytes 12292
  158.7 48.3 %copy-start.29 = (f32[1024]{0:T(1024)S(1)}, f32[1024]{0:T(1024)}, u32[]{:S(2)}) copy-start(f32[1024]{0:T(1024)} %param.37) | copy-start | bytes 12292
  158.7 49.0 %copy-start.32 = (f32[1024]{0:T(1024)S(1)}, f32[1024]{0:T(1024)}, u32[]{:S(2)}) copy-start(f32[1024]{0:T(1024)} %param.38) | copy-start | bytes 12292
  158.8 74.1 %all-gather.9.cloned.1.call-start = ((), (), s32[]{:S(2)}) async-start(), calls=%async_computation.8 | async-start | bytes 2785280 | tf_op jit(solution)/shard_map/all_gather | solution.py:188
  209.4 83.7 %reduce-scatter.9.cloned.1.call-start = ((), (), s32[]{:S(2)}) async-start(), calls=%async_computation.9 | async-start | bytes 5570560 | tf_op jit(solution)/shard_map/reduce_scatter | solution.py:194
  232.9 9.1 %copy-start.39 = (bf16[1024,1024]{1,0:T(8,128)(2,1)S(1)}, bf16[1024,1024]{1,0:T(8,128)(2,1)}, u32[]{:S(2)}) copy-start(bf16[1024,1024]{1,0:T(8,128)(2,1)} %param.33) | copy-start | bytes 6291460
  246.6 48.2 %copy-start.3 = (f32[272,1024]{1,0:T(8,128)S(1)}, f32[272,1024]{1,0:T(8,128)}, u32[]{:S(2)}) copy-start(f32[272,1024]{1,0:T(8,128)} %reduce-scatter.5.cloned.1.call-done) | copy-start | bytes 3342340
  246.7 48.2 %copy-start.10 = (bf16[272,1024]{1,0:T(8,128)(2,1)S(1)}, bf16[272,1024]{1,0:T(8,128)(2,1)}, u32[]{:S(2)}) copy-start(bf16[272,1024]{1,0:T(8,128)(2,1)} %param.39) | copy-start | bytes 1671172
  246.7 75.3 %all-gather.11.cloned.1.call-start = ((), (), s32[]{:S(2)}) async-start(), calls=%async_computation.10 | async-start | bytes 2785280 | tf_op jit(solution)/shard_map/all_gather | solution.py:206
  297.2 24.8 %copy-start.19 = (bf16[256,1024]{1,0:T(8,128)(2,1)S(1)}, bf16[256,1024]{1,0:T(8,128)(2,1)}, u32[]{:S(2)}) copy-start(bf16[256,1024]{1,0:T(8,128)(2,1)} %param.27) | copy-start | bytes 1572868
  298.5 154.6 %reduce-scatter.11.cloned.1.call-start = ((), (), s32[]{:S(2)}) async-start(), calls=%async_computation.11 | async-start | bytes 5570560 | tf_op jit(solution)/shard_map/reduce_scatter | solution.py:219
  406.7 448.0 %all-reduce.5.cloned.1.call-start = ((), (), s32[]{:S(2)}) async-start(), calls=%async_computation.12 | async-start | bytes 25165824 | tf_op jit(solution)/shard_map/psum | solution.py:252
  406.9 7.4 copy-start.37
  414.3 8.7 copy-start.16
  414.3 8.7 copy-start.38
  414.3 10.5 %copy-start.36 = (bf16[1088,1024]{1,0:T(8,128)(2,1)S(1)}, bf16[1088,1024]{1,0:T(8,128)(2,1)}, u32[]{:S(2)}) copy-start(bf16[1088,1024]{1,0:T(8,128)(2,1)} %all-gather.5.cloned.1.call-done) | copy-start | bytes 6684676
  428.8 24.3 %copy-start.5 = (bf16[272,1024]{1,0:T(8,128)(2,1)S(1)}, bf16[272,1024]{1,0:T(8,128)(2,1)}, u32[]{:S(2)}) copy-start(bf16[272,1024]{1,0:T(8,128)(2,1)} %param.20) | copy-start | bytes 1671172
  428.8 24.3 %copy-start.23 = (f32[272]{0:T(512)S(1)}, f32[272]{0:T(512)}, u32[]{:S(2)}) copy-start(f32[272]{0:T(512)} %copy-done.22) | copy-start | bytes 3268
  428.8 24.3 %copy-start.24 = (f32[1024]{0:T(1024)S(1)}, f32[1024]{0:T(1024)}, u32[]{:S(2)}) copy-start(f32[1024]{0:T(1024)} %param.22) | copy-start | bytes 12292
  428.8 24.3 %copy-start.28 = (f32[272]{0:T(512)S(1)}, f32[272]{0:T(512)}, u32[]{:S(2)}) copy-start(f32[272]{0:T(512)} %copy-done.27) | copy-start | bytes 3268
  428.8 70.6 %copy-start.8 = (f32[272,1024]{1,0:T(8,128)S(1)}, f32[272,1024]{1,0:T(8,128)}, u32[]{:S(2)}) copy-start(f32[272,1024]{1,0:T(8,128)} %copy-done.7) | copy-start | bytes 3342340
  (20 other events, 38.3 us)
Sparse Core Ops, SparseCore 0:
  12.9 26.0 all-gather.4
  73.4 46.2 reduce-scatter.4
  123.6 23.2 all-gather.6
  158.9 46.2 reduce-scatter.6
  209.5 23.2 all-gather.8
  246.8 46.2 reduce-scatter.8
  298.7 23.2 all-gather.10
  406.8 46.2 reduce-scatter.10
  459.0 395.6 all-reduce.4
where the time goes:
time: 882 us; the launch traced here: 873 us
  waiting for transfers between devices  578 us (66%)
  matrix products  158 us (18%)
  blocking collectives  66.8 us (8%)
  other arithmetic  24.3 us (3%)
  local copies, waits for them, and re-layouts  19.3 us (2%)
  between operations  15.1 us (2%)
  starting transfers between devices  11.1 us (1%)
    psum x1, waiting for transfers between devices, local(): lax.psum((part_qkv, part_q_bias, part_v_bias, part_out, ffn_fc1, ffn_fc1_...  353 us
    reduce_scatter x1, waiting for transfers between devices, local(): lax.psum_scatter(times_transposed(grad_inner, w_fc1), 'tensor', scatter_d...  46.4 us
    reduce_scatter x1, waiting for transfers between devices, local(): lax.psum_scatter(jnp.dot(activated, w_fc2, preferred_element_type=jnp.flo...  46.3 us
    psum x1, blocking collectives, local(): lax.psum((grad_gain1, grad_shift1, grad_gain2, grad_shift2, grad_gain3, g...  44.4 us
    reduce_scatter x1, waiting for transfers between devices, local(): lax.psum_scatter(jnp.dot(context_low, w_out, preferred_element_type=jnp.f...  36.2 us
    dot_general x1, matrix products, attend_backward(): jnp.einsum('hqk,khd->qhd', grad_scores, key_rows, preferred_element_type=...  27.5 us
    dot_general x1, matrix products, attend_backward(): jnp.einsum('hqk,qhd->khd', grad_scores, query_rows, preferred_element_typ...  26.3 us
    all_gather x1, waiting for transfers between devices, local(): lax.all_gather(first_out.astype(jnp.bfloat16), 'tensor', axis=0, tiled=True)  24.9 us
  transfers between devices with their start and end apart: 9, of which 9 were waited for; matrix products, arithmetic and copies ran while one was open for 3% of the time, Pallas kernels for 0%

commit v1 on v0

--- a/solution.py
+++ b/solution.py
@@ -43,6 +43,12 @@
         - normed * jnp.mean(scaled * normed, axis=-1, keepdims=True)
     )
     return (inner_term * inverse, jnp.sum(grad_out * normed, axis=0), jnp.sum(grad_out, axis=0))
+
+
+def scatter_low(partial_sums):
+    return lax.psum_scatter(
+        partial_sums.astype(jnp.bfloat16), "tensor", scatter_dimension=0, tiled=True
+    ).astype(jnp.float32)
 
 
 def gelu_back(inner_act, grad_act):
@@ -153,12 +159,7 @@
     )
     context_low = context.reshape(rows_all, local_heads * HD).astype(jnp.bfloat16)
     branch = (
-        lax.psum_scatter(
-            jnp.dot(context_low, w_out, preferred_element_type=jnp.float32),
-            "tensor",
-            scatter_dimension=0,
-            tiled=True,
-        )
+        scatter_low(jnp.dot(context_low, w_out, preferred_element_type=jnp.float32))
         + out_bias
     )
     second_out, second_hat, second_inv = norm_forward(branch, norm2_gain, norm2_shift)
@@ -169,12 +170,7 @@
     inner_act = jnp.dot(gathered_third, w_fc1, preferred_element_type=jnp.float32) + fc1_bias
     activated = jax.nn.gelu(inner_act, approximate=True).astype(jnp.bfloat16)
     mixed_out = (
-        lax.psum_scatter(
-            jnp.dot(activated, w_fc2, preferred_element_type=jnp.float32),
-            "tensor",
-            scatter_dimension=0,
-            tiled=True,
-        )
+        scatter_low(jnp.dot(activated, w_fc2, preferred_element_type=jnp.float32))
         + fc2_bias
     )
     fourth_out, fourth_hat, fourth_inv = norm_forward(mixed_out, norm4_gain, norm4_shift)
@@ -191,9 +187,7 @@
     grad_inner = gelu_back(inner_act, grad_activated).astype(jnp.bfloat16)
     ffn_fc1_bias = jnp.sum(grad_inner, axis=0, dtype=jnp.float32)
     ffn_fc1 = transposed_times(gathered_third, grad_inner)
-    grad_third = lax.psum_scatter(
-        times_transposed(grad_inner, w_fc1), "tensor", scatter_dimension=0, tiled=True
-    )
+    grad_third = scatter_low(times_transposed(grad_inner, w_fc1))
     grad_mid_norm, grad_gain3, grad_shift3 = norm_backward(
         grad_third, third_hat, third_inv, norm3_gain
     )
@@ -216,13 +210,30 @@
         rows_all, 3 * local_heads * HD
     )
     part_qkv = transposed_times(gathered_first, grad_projected)
-    grad_first = lax.psum_scatter(
-        times_transposed(grad_projected, w_qkv), "tensor", scatter_dimension=0, tiled=True
-    )
+    grad_first = scatter_low(times_transposed(grad_projected, w_qkv))
     grad_input_norm, grad_gain1, grad_shift1 = norm_backward(
         grad_first, first_hat, first_inv, norm1_gain
     )
     input_grad = grad_hidden + grad_input_norm
+    shared = jnp.concatenate(
+        [
+            grad_gain1,
+            grad_shift1,
+            grad_gain2,
+            grad_shift2,
+            grad_gain3,
+            grad_shift3,
+            grad_gain4,
+            grad_shift4,
+            grad_out_bias,
+            grad_fc2_bias,
+        ]
+    )
+    owned = jnp.concatenate([part_q_bias, part_v_bias, ffn_fc1_bias])
+    places = lax.axis_size("tensor")
+    slots = jnp.zeros((places, owned.shape[0]), jnp.float32)
+    slots = lax.dynamic_update_slice(slots, owned[None], (lax.axis_index("tensor"), 0))
+    small = lax.psum(jnp.concatenate([shared, slots.reshape(-1)]), ("dp", "tensor"))
     (
         grad_gain1,
         grad_shift1,
@@ -234,23 +245,19 @@
         grad_shift4,
         grad_out_bias,
         grad_fc2_bias,
-    ) = lax.psum(
-        (
-            grad_gain1,
-            grad_shift1,
-            grad_gain2,
-            grad_shift2,
-            grad_gain3,
-            grad_shift3,
-            grad_gain4,
-            grad_shift4,
-            grad_out_bias,
-            grad_fc2_bias,
-        ),
-        ("dp", "tensor"),
-    )
-    part_qkv, part_q_bias, part_v_bias, part_out, ffn_fc1, ffn_fc1_bias, ffn_fc2 = lax.psum(
-        (part_qkv, part_q_bias, part_v_bias, part_out, ffn_fc1, ffn_fc1_bias, ffn_fc2), "dp"
+    ) = small[: shared.shape[0]].reshape(10, -1)
+    mine = lax.dynamic_slice(
+        small, (shared.shape[0] + lax.axis_index("tensor") * owned.shape[0],), owned.shape
+    )
+    part_q_bias, part_v_bias, ffn_fc1_bias = jnp.split(
+        mine, [part_q_bias.shape[0], part_q_bias.shape[0] + part_v_bias.shape[0]]
+    )
+    part_qkv, part_out, ffn_fc1, ffn_fc2 = (
+        total.astype(jnp.float32)
+        for total in lax.psum(
+            tuple(part.astype(jnp.bfloat16) for part in (part_qkv, part_out, ffn_fc1, ffn_fc2)),
+            "dp",
+        )
     )
     return (
         layer_out,

time: 882 us -> 767 us (0.87)
  blocking collectives: 66.8 us -> 0 us
  waiting for transfers between devices: 578 us -> 536 us
  other arithmetic: 24.3 us -> 38 us
  starting transfers between devices: 11.1 us -> 1.51 us
    psum x2 -> x0, blocking collectives: 66.8 us -> none  [the longest x1 44.4 us: local(): lax.psum((grad_gain1, grad_shift1, grad_gain2, grad_shift2, grad_gain3, g...]
    psum x1 -> x2, waiting for transfers between devices: 353 us -> 332 us  [the longest x1 214 us: local(): lax.psum(tuple((part.astype(jnp.bfloat16) for part in (part_qkv, part_out...]
    reduce_scatter x4, waiting for transfers between devices: 131 us -> 110 us  [scatter_low(): lax.psum_scatter(partial_sums.astype(jnp.bfloat16), 'tensor', scatter_dim...]
    unnamed x90 -> x94, local copies, waits for them, and re-layouts: 18.6 us -> 8.56 us
    all_gather x1, starting transfers between devices: 10.2 us -> 0.51 us  [local(): gathered_third = lax.all_gather(third_low, 'tensor', axis=0, tiled=True)]
    convert_element_type x0 -> x4, other arithmetic: none -> 9.1 us  [local(): total.astype(jnp.float32)]
  transfers between devices with their start and end apart: 9 -> 10, of which waited for: 9 -> 10; matrix products, arithmetic and copies ran while one was open for 3% -> 3% of each run, Pallas kernels for 0% -> 0%
where the time goes in v1:
time: 767 us; the launch traced here: 758 us
  waiting for transfers between devices  536 us (70%)
  matrix products  155 us (20%)
  other arithmetic  38 us (5%)
  between operations  15.8 us (2%)
  local copies, waits for them, and re-layouts  12.3 us (2%)
    psum x1, waiting for transfers between devices, local(): lax.psum(tuple((part.astype(jnp.bfloat16) for part in (part_qkv, part_out...  214 us
    psum x1, waiting for transfers between devices, local(): lax.psum(jnp.concatenate([shared, slots.reshape(-1)]), ('dp', 'tensor'))  117 us
    reduce_scatter x4, waiting for transfers between devices, scatter_low(): lax.psum_scatter(partial_sums.astype(jnp.bfloat16), 'tensor', scatter_dim...  110 us
    dot_general x1, matrix products, attend_backward(): jnp.einsum('hqk,khd->qhd', grad_scores, key_rows, preferred_element_type=...  27.5 us
    dot_general x1, matrix products, attend_backward(): jnp.einsum('hqk,qhd->khd', grad_scores, query_rows, preferred_element_typ...  26.3 us
    all_gather x1, waiting for transfers between devices, local(): lax.all_gather(first_out.astype(jnp.bfloat16), 'tensor', axis=0, tiled=True)  23.9 us
    all_gather x1, waiting for transfers between devices, local(): gathered_third = lax.all_gather(third_low, 'tensor', axis=0, tiled=True)  23.4 us
    all_gather x1, waiting for transfers between devices, local(): gathered_grad = lax.all_gather(mixed_low, 'tensor', axis=0, tiled=True)  23.2 us
  transfers between devices with their start and end apart: 10, of which 10 were waited for; matrix products, arithmetic and copies ran while one was open for 3% of the time, Pallas kernels for 0%

profile of v1, /device:TPU:0, one launch (start us, length us, event | category | flops | bytes accessed | tf_op | source)
XLA Modules:
  0.0 758.3 jit_solution(13749449634654296222)
XLA Ops:
  10.0 2.2 fusion.63
  14.5 23.9 %all-gather.5.cloned.1.call-done = bf16[1088,1024]{1,0:T(8,128)(2,1)} async-done(((bf16[272,1024]{1,0:T(8,128)(2,1)}), bf16[1088,1024]{1,0:T(8,128)(2,1)}) %all-gather.5.cloned.1.call-update) | async-done | bytes 2228240 | tf_op jit(solution)/shard_map/all_gather | solution.py:141
  38.4 6.1 fusion.110
  44.6 16.7 %fusion.103 = (f32[4,1088]{1,0:T(4,128)S(1)}, f32[4,1088,1088]{1,2,0:T(8,128)}) fusion(pred[1088,1088]{0,1:T(8,128)(4,1)} %fusion.22, f32[1088,4,3,64]{0,3,2,1:T(8,128)} %bitcast.78, f32[4,64]{1,0:T(4,128)S(1)} %add.165), kind=kOutput, calls=%fused_computation.162 | convolution fusion | flops 635044928 | bytes 23234560 | tf_op jit(solution)/shard_map/while/body/eval_jaxpr/sub | solution.py:75
  61.2 9.0 %fusion.30 = bf16[4,64,1088]{2,1,0:T(8,128)(2,1)S(1)} fusion(f32[1088,4,3,64]{0,3,2,1:T(8,128)} %bitcast.79, f32[4,64]{1,0:T(4,128)S(1)} %add.162, f32[4,1088,1088]{1,2,0:T(8,128)} %get-tuple-element.118, f32[4,1088]{1,0:T(4,128)S(1)} %get-tuple-element.117), kind=kOutput, calls=%fused_computation.39 | convolution fusion | flops 616382464 | bytes 21809152 | tf_op jit(solution)/shard_map/while/body/eval_jaxpr/hqk,khd->qhd/dot_general | solution.py:78
  73.8 31.6 %reduce-scatter.5.cloned.1.call-done = bf16[272,1024]{1,0:T(8,128)(2,1)} async-done(((bf16[1088,1024]{1,0:T(8,128)(2,1)}), bf16[272,1024]{1,0:T(8,128)(2,1)}) %reduce-scatter.5.cloned.1.call-update) | async-done | bytes 557072 | tf_op jit(solution)/shard_map/reduce_scatter | solution.py:49
  112.1 23.4 %all-gather.7.cloned.1.call-done = bf16[1088,1024]{1,0:T(8,128)(2,1)} async-done(((bf16[272,1024]{1,0:T(8,128)(2,1)}), bf16[1088,1024]{1,0:T(8,128)(2,1)}) %all-gather.7.cloned.1.call-update) | async-done | bytes 2228240 | tf_op jit(solution)/shard_map/all_gather | solution.py:169
  135.5 4.7 convolution_add_fusion
  142.3 4.2 convolution_convert_fusion.2
  146.6 32.1 %reduce-scatter.7.cloned.1.call-done = bf16[272,1024]{1,0:T(8,128)(2,1)} async-done(((bf16[1088,1024]{1,0:T(8,128)(2,1)}), bf16[272,1024]{1,0:T(8,128)(2,1)}) %reduce-scatter.7.cloned.1.call-update) | async-done | bytes 557072 | tf_op jit(solution)/shard_map/reduce_scatter | solution.py:49
  184.8 23.2 %all-gather.9.cloned.1.call-done = bf16[1088,1024]{1,0:T(8,128)(2,1)} async-done(((bf16[272,1024]{1,0:T(8,128)(2,1)}), bf16[1088,1024]{1,0:T(8,128)(2,1)}) %all-gather.9.cloned.1.call-update) | async-done | bytes 2228240 | tf_op jit(solution)/shard_map/all_gather | solution.py:184
  208.1 7.8 %convert_reduce_fusion = (f32[1024]{0:T(1024)S(1)}, bf16[1088,1024]{1,0:T(8,128)(2,1)S(1)}) fusion(f32[1088,1024]{1,0:T(8,128)} %copy-done.38, bf16[1088,1024]{1,0:T(8,128)(2,1)} %all-gather.9.cloned.1.call-done, bf16[1024,1024]{1,0:T(8,128)(2,1)S(1)} %copy-done), kind=kOutput, calls=%fused_computation.33 | convolution fusion | flops 2306210816 | bytes 11014144 | tf_op jit(solution)/shard_map/dot_general | solution.py:19
  217.2 3.9 convolution_convert_fusion.1
  221.2 32.1 %reduce-scatter.9.cloned.1.call-done = bf16[272,1024]{1,0:T(8,128)(2,1)} async-done(((bf16[1088,1024]{1,0:T(8,128)(2,1)}), bf16[272,1024]{1,0:T(8,128)(2,1)}) %reduce-scatter.9.cloned.1.call-update) | async-done | bytes 557072 | tf_op jit(solution)/shard_map/reduce_scatter | solution.py:49
  253.3 3.2 fusion.76
  259.3 23.2 %all-gather.11.cloned.1.call-done = bf16[1088,1024]{1,0:T(8,128)(2,1)} async-done(((bf16[272,1024]{1,0:T(8,128)(2,1)}), bf16[1088,1024]{1,0:T(8,128)(2,1)}) %all-gather.11.cloned.1.call-update) | async-done | bytes 2228240 | tf_op jit(solution)/shard_map/all_gather | solution.py:200
  282.5 2.4 convolution_convert_fusion.4
  285.2 9.8 %convert_reduce_fusion.5 = (f32[4,64]{1,0:T(4,128)S(1)}, bf16[4,64,1088]{2,1,0:T(8,128)(2,1)S(1)}) fusion(bf16[1088,4,64]{0,2,1:T(8,128)(2,1)S(1)} %bitcast.70, f32[4,1088,1088]{1,2,0:T(8,128)} %get-tuple-element.118, f32[4,1088]{1,0:T(4,128)S(1)} %get-tuple-element.117), kind=kOutput, calls=%fused_computation.83 | convolution fusion | flops 616382208 | bytes 20072448 | tf_op jit(solution)/shard_map/while/body/eval_jaxpr/hqk,qhd->khd/dot_general | solution.py:88
  295.0 10.9 %fusion.88 = f32[4,1088,1088]{1,2,0:T(8,128)} fusion(bf16[1088,4,64]{0,2,1:T(8,128)(2,1)S(1)} %bitcast.71, f32[1088,4,3,64]{0,3,2,1:T(8,128)} %bitcast.80, f32[4,64]{1,0:T(4,128)S(1)} %add.162), kind=kOutput, calls=%fused_computation.123 | convolution fusion | flops 606633984 | bytes 20677632 | tf_op jit(solution)/shard_map/while/body/eval_jaxpr/qhd,khd->hqk/dot_general | solution.py:94
  305.9 26.3 %fusion.42 = bf16[1,1088,4,1,64]{1,4,2,3,0:T(8,128)(2,1)S(1)} fusion(f32[4,1088,1088]{1,2,0:T(8,128)} %fusion.88, f32[1088,4,3,64]{0,3,2,1:T(8,128)} %bitcast.81, f32[4,64]{1,0:T(4,128)S(1)} %add.165, f32[4,1088,1088]{1,2,0:T(8,128)} %get-tuple-element.118, f32[4,1088]{1,0:T(4,128)S(1)} %get-tuple-element.117), kind=kOutput, calls=%fused_computation.44 | convolution fusion | flops 640062784 | bytes 81991680 | tf_op jit(solution)/shard_map/while/body/eval_jaxpr/hqk,qhd->khd/dot_general | solution.py:104
  332.2 27.5 %convert_reduce_fusion.6 = (f32[4,64]{1,0:T(4,128)S(1)}, bf16[4,64,1088]{2,1,0:T(8,128)(2,1)}) fusion(f32[4,1088,1088]{1,2,0:T(8,128)} %fusion.88, f32[4,1088,1088]{1,2,0:T(8,128)} %get-tuple-element.118, f32[4,1088]{1,0:T(4,128)S(1)} %get-tuple-element.117, f32[1088,4,3,64]{0,3,2,1:T(8,128)} %bitcast.82), kind=kOutput, calls=%fused_computation.84 | convolution fusion | flops 640062528 | bytes 81400832 | tf_op jit(solution)/shard_map/while/body/eval_jaxpr/hqk,khd->qhd/dot_general | solution.py:101
  363.0 3.5 convolution_convert_fusion
  366.9 6.7 convolution_convert_fusion.6
  373.6 4.4 convolution_convert_fusion.5
  378.4 5.7 convolution_convert_fusion.7
  384.0 14.7 %reduce-scatter.11.cloned.1.call-done = bf16[272,1024]{1,0:T(8,128)(2,1)} async-done(((bf16[1088,1024]{1,0:T(8,128)(2,1)}), bf16[272,1024]{1,0:T(8,128)(2,1)}) %reduce-scatter.11.cloned.1.call-update) | async-done | bytes 557072 | tf_op jit(solution)/shard_map/reduce_scatter | solution.py:49
  401.2 3.3 convolution_convert_fusion.8
  407.0 117.2 %all-reduce.4.cloned.1.call-done = f32[16384]{0:T(1024)} async-done(((f32[16384]{0:T(1024)}), f32[16384]{0:T(1024)}) %all-reduce.4.cloned.1.call-update) | async-done | bytes 65552 | tf_op jit(solution)/shard_map/psum | solution.py:236
  527.0 214.3 %all-reduce.6.cloned.1.call-done = (bf16[1024,768]{1,0:T(8,128)(2,1)}, bf16[256,1024]{1,0:T(8,128)(2,1)}, bf16[1024,1024]{1,0:T(8,128)(2,1)}, bf16[1024,1024]{1,0:T(8,128)(2,1)}) async-done(((bf16[1024,768]{1,0:T(8,128)(2,1)}, bf16[256,1024]{1,0:T(8,128)(2,1)}, bf16[1024,1024]{1,0:T(8,128)(2,1)}, bf16[1024,1024]{1,0:T(8,128)(2,1)}), (bf16[1024,768]{1,0:T(8,128)(2,1)}, bf16[256,1024]{1,0:T(8,128)(2,1)}, ...) | async-done | bytes 6291472 | tf_op jit(solution)/shard_map/psum | solution.py:257
  741.3 2.2 convert_element_type.189
  746.1 2.5 convert_element_type.191
  748.6 2.5 convert_element_type.193
  (165 shorter events, 41.6 us)
Async XLA Ops:
  7.2 135.1 %copy-start = (bf16[1024,1024]{1,0:T(8,128)(2,1)S(1)}, bf16[1024,1024]{1,0:T(8,128)(2,1)}, u32[]{:S(2)}) copy-start(bf16[1024,1024]{1,0:T(8,128)(2,1)} %param.35) | copy-start | bytes 6291460
  7.2 31.2 %all-gather.5.cloned.1.call-start = ((), (), s32[]{:S(2)}) async-start(), calls=%async_computation.4 | async-start | bytes 2785280 | tf_op jit(solution)/shard_map/all_gather | solution.py:141
  10.0 34.5 %copy-start.28 = (f32[272]{0:T(512)}, f32[272]{0:T(512)S(1)}, u32[]{:S(2)}) copy-start(f32[272]{0:T(512)S(1)} %add_rsqrt_fusion.3) | copy-start | bytes 3268
  12.2 93.1 %reduce-scatter.5.cloned.1.call-start = ((), (), s32[]{:S(2)}) async-start(), calls=%async_computation.5 | async-start | bytes 2785280 | tf_op jit(solution)/shard_map/reduce_scatter | solution.py:49
  61.2 9.8 %copy-start.16 = (bf16[256,1024]{1,0:T(8,128)(2,1)S(1)}, bf16[256,1024]{1,0:T(8,128)(2,1)}, u32[]{:S(2)}) copy-start(bf16[256,1024]{1,0:T(8,128)(2,1)} %param.27) | copy-start | bytes 1572868
  73.2 32.2 %copy-start.18 = (f32[1024]{0:T(1024)S(1)}, f32[1024]{0:T(1024)}, u32[]{:S(2)}) copy-start(f32[1024]{0:T(1024)} %param.28) | copy-start | bytes 12292
  73.2 34.9 %copy-start.2 = (bf16[272,1024]{1,0:T(8,128)(2,1)S(1)}, bf16[272,1024]{1,0:T(8,128)(2,1)}, u32[]{:S(2)}) copy-start(bf16[272,1024]{1,0:T(8,128)(2,1)} %param.20) | copy-start | bytes 1671172
  73.2 34.9 %copy-start.19 = (f32[1024]{0:T(1024)S(1)}, f32[1024]{0:T(1024)}, u32[]{:S(2)}) copy-start(f32[1024]{0:T(1024)} %param.29) | copy-start | bytes 12292
  73.2 34.9 %copy-start.21 = (f32[1024]{0:T(1024)S(1)}, f32[1024]{0:T(1024)}, u32[]{:S(2)}) copy-start(f32[1024]{0:T(1024)} %param.30) | copy-start | bytes 12292
  73.2 37.1 %copy-start.26 = (f32[1024]{0:T(1024)S(1)}, f32[1024]{0:T(1024)}, u32[]{:S(2)}) copy-start(f32[1024]{0:T(1024)} %param.31) | copy-start | bytes 12292
  73.2 37.1 %copy-start.30 = (f32[1024]{0:T(1024)S(1)}, f32[1024]{0:T(1024)}, u32[]{:S(2)}) copy-start(f32[1024]{0:T(1024)} %param.32) | copy-start | bytes 12292
  73.2 62.2 %all-gather.7.cloned.1.call-start = ((), (), s32[]{:S(2)}) async-start(), calls=%async_computation.6 | async-start | bytes 2785280 | tf_op jit(solution)/shard_map/all_gather | solution.py:169
  112.0 66.6 %reduce-scatter.7.cloned.1.call-start = ((), (), s32[]{:S(2)}) async-start(), calls=%async_computation.7 | async-start | bytes 2785280 | tf_op jit(solution)/shard_map/reduce_scatter | solution.py:49
  146.5 32.2 %copy-start.20 = (f32[1024]{0:T(1024)S(1)}, f32[1024]{0:T(1024)}, u32[]{:S(2)}) copy-start(f32[1024]{0:T(1024)} %param.36) | copy-start | bytes 12292
  146.5 34.9 %copy-start.25 = (f32[1024]{0:T(1024)S(1)}, f32[1024]{0:T(1024)}, u32[]{:S(2)}) copy-start(f32[1024]{0:T(1024)} %param.37) | copy-start | bytes 12292
  146.5 61.5 %all-gather.9.cloned.1.call-start = ((), (), s32[]{:S(2)}) async-start(), calls=%async_computation.8 | async-start | bytes 2785280 | tf_op jit(solution)/shard_map/all_gather | solution.py:184
  184.6 68.7 %reduce-scatter.9.cloned.1.call-start = ((), (), s32[]{:S(2)}) async-start(), calls=%async_computation.9 | async-start | bytes 2785280 | tf_op jit(solution)/shard_map/reduce_scatter | solution.py:49
  208.1 9.1 %copy-start.36 = (bf16[1024,1024]{1,0:T(8,128)(2,1)S(1)}, bf16[1024,1024]{1,0:T(8,128)(2,1)}, u32[]{:S(2)}) copy-start(bf16[1024,1024]{1,0:T(8,128)(2,1)} %param.33) | copy-start | bytes 6291460
  221.1 32.2 %copy-start.5 = (bf16[272,1024]{1,0:T(8,128)(2,1)S(1)}, bf16[272,1024]{1,0:T(8,128)(2,1)}, u32[]{:S(2)}) copy-start(bf16[272,1024]{1,0:T(8,128)(2,1)} %reduce-scatter.7.cloned.1.call-done) | copy-start | bytes 1671172
  221.1 32.2 %copy-start.31 = (f32[1024]{0:T(1024)S(1)}, f32[1024]{0:T(1024)}, u32[]{:S(2)}) copy-start(f32[1024]{0:T(1024)} %param.38) | copy-start | bytes 12292
  221.1 35.3 %copy-start.7 = (bf16[272,1024]{1,0:T(8,128)(2,1)S(1)}, bf16[272,1024]{1,0:T(8,128)(2,1)}, u32[]{:S(2)}) copy-start(bf16[272,1024]{1,0:T(8,128)(2,1)} %param.39) | copy-start | bytes 1671172
  221.1 61.4 %all-gather.11.cloned.1.call-start = ((), (), s32[]{:S(2)}) async-start(), calls=%async_computation.10 | async-start | bytes 2785280 | tf_op jit(solution)/shard_map/all_gather | solution.py:200
  257.7 24.8 %copy-start.17 = (bf16[256,1024]{1,0:T(8,128)(2,1)S(1)}, bf16[256,1024]{1,0:T(8,128)(2,1)}, u32[]{:S(2)}) copy-start(bf16[256,1024]{1,0:T(8,128)(2,1)} %param.27) | copy-start | bytes 1572868
  259.0 139.7 %reduce-scatter.11.cloned.1.call-start = ((), (), s32[]{:S(2)}) async-start(), calls=%async_computation.11 | async-start | bytes 2785280 | tf_op jit(solution)/shard_map/reduce_scatter | solution.py:49
  363.0 10.6 %slice-start = ((s8[4456448]{0:T(1024)(128)(4,1)}), s8[262144]{0:T(1024)(128)(4,1)S(1)}, s32[]{:S(2)}) async-start(s8[4456448]{0:T(1024)(128)(4,1)} %bitcast.83), calls=%async_computation.14 | async-start | bytes 524288
  366.5 157.7 %all-reduce.4.cloned.1.call-start = ((), (), s32[]{:S(2)}) async-start(), calls=%async_computation.12 | async-start | bytes 131072 | tf_op jit(solution)/shard_map/psum | solution.py:236
  366.9 6.7 copy-start.35
  378.3 20.4 %copy-start.24 = (f32[272]{0:T(512)S(1)}, f32[272]{0:T(512)}, u32[]{:S(2)}) copy-start(f32[272]{0:T(512)} %copy-done.23) | copy-start | bytes 3268
  378.3 20.4 %copy-start.27 = (f32[1024]{0:T(1024)S(1)}, f32[1024]{0:T(1024)}, u32[]{:S(2)}) copy-start(f32[1024]{0:T(1024)} %param.22) | copy-start | bytes 12292
  378.3 20.4 %copy-start.29 = (f32[272]{0:T(512)S(1)}, f32[272]{0:T(512)}, u32[]{:S(2)}) copy-start(f32[272]{0:T(512)} %copy-done.28) | copy-start | bytes 3268
  378.4 22.9 %copy-start.15 = (bf16[4,64,1088]{2,1,0:T(8,128)(2,1)S(1)}, bf16[4,64,1088]{2,1,0:T(8,128)(2,1)}, u32[]{:S(2)}) copy-start(bf16[4,64,1088]{2,1,0:T(8,128)(2,1)} %copy-done.14) | copy-start | bytes 1671172
  401.2 340.1 %all-reduce.6.cloned.1.call-start = ((), (), s32[]{:S(2)}) async-start(), calls=%async_computation.13 | async-start | bytes 12582912 | tf_op jit(solution)/shard_map/psum | solution.py:257
  (20 other events, 62.2 us)
Sparse Core Ops, SparseCore 0:
  12.3 26.0 all-gather.4
  73.3 31.9 reduce-scatter.4
  112.1 23.2 all-gather.6
  146.6 31.9 reduce-scatter.6
  184.7 23.2 all-gather.8
  221.2 31.9 reduce-scatter.8
  259.2 23.2 all-gather.10
  366.7 31.9 reduce-scatter.10
  404.9 119.2 all-reduce.3
  529.7 211.5 all-reduce.5
